TPU v7x, 32 devices: a whole 2x2x4 slice. The times are simulated.
32 devices in a mesh: lat: 4 (over x, core), lon: 8 (over z, y).
Axes of the slice: x: 2, y: 2, z: 4, core: 2. Of those that a mesh axis runs over, the one named last changes fastest.
Arguments:
- tokens: bfloat16 [4, 48, 96, 512], P(None, 'lat', 'lon'), may hold values from -6 to 6
- region: int32 [4, 48, 96], P(None, 'lat', 'lon'), may hold values from 0 to 2
- norm_gain1: float32 [2, 512], replicated, may hold values from 0.25 to 1.75
- qkv_weight: bfloat16 [2, 512, 1536], replicated, may hold values from -3 to 3
- proj_weight: bfloat16 [2, 512, 512], replicated, may hold values from -0.25 to 0.25
- norm_gain2: float32 [2, 512], replicated, may hold values from 0.25 to 1.75
- up_weight: bfloat16 [2, 512, 2048], replicated, may hold values from -0.25 to 0.25
- down_weight: bfloat16 [2, 2048, 512], replicated, may hold values from -0.125 to 0.125
Outputs:
- result: bfloat16 [4, 48, 96, 512], P(None, 'lat', 'lon')
All inputs are finite; a program needn't handle non-finite values.
Results may differ from a plain program's by a relative error of at most 0.012.
Values may be sent and summed in bfloat16 or wider, within the bound.
A program may use at most 64 MiB of HBM per device.

v0:
```python
import math

import jax
import jax.numpy as jnp
from jax import lax
from jax.sharding import PartitionSpec as P

HEADS = 8
WLEV = 2
WLAT = 6
WLON = 12


epsilon = 1e-05


def shifted_2(value, axis, steps):
    count = lax.axis_size(axis)
    pairs = [(source, (source + steps) % count) for source in range(count)]
    return lax.ppermute(value, axis, pairs)


def layer_norm(field, gain_vector):
    field = field.astype(jnp.float32)
    average = jnp.mean(field, axis=-1, keepdims=True)
    centered = field - average
    variance = jnp.mean(centered * centered, axis=-1, keepdims=True)
    return centered * lax.rsqrt(variance + epsilon) * gain_vector


def to_windows(field):
    level_count, row_count, column_count = field.shape[:3]
    trailing = tuple(field.shape[3:])
    shaped = field.reshape(
        (level_count // WLEV, WLEV, row_count // WLAT, WLAT, column_count // WLON, WLON) + trailing
    )
    order = (0, 2, 4, 1, 3, 5) + tuple(range(6, 6 + len(trailing)))
    return jnp.transpose(shaped, order).reshape((-1, WLEV * WLAT * WLON) + trailing)


def from_windows(windows, level_count, row_count, column_count):
    trailing = tuple(windows.shape[2:])
    shaped = windows.reshape(
        (level_count // WLEV, row_count // WLAT, column_count // WLON, WLEV, WLAT, WLON) + trailing
    )
    order = (0, 3, 1, 4, 2, 5) + tuple(range(6, 6 + len(trailing)))
    return jnp.transpose(shaped, order).reshape((level_count, row_count, column_count) + trailing)


def window_attention(normed, labels, w_qkv, w_proj):
    count, span, features = normed.shape
    head_size = features // HEADS
    mixed = jnp.dot(normed, w_qkv, preferred_element_type=jnp.float32).astype(jnp.bfloat16)
    queries = mixed[..., :features].reshape(count, span, HEADS, head_size)
    key_vectors = mixed[..., features : 2 * features].reshape(count, span, HEADS, head_size)
    values = mixed[..., 2 * features :].reshape(count, span, HEADS, head_size)
    scores = jnp.einsum("wqhd,wkhd->whqk", queries, key_vectors, preferred_element_type=jnp.float32)
    scores = scores * (1.0 / math.sqrt(head_size))
    allowed = labels[:, None, :, None] == labels[:, None, None, :]
    scores = jnp.where(allowed, scores, -jnp.inf)
    peak = jnp.max(scores, axis=-1, keepdims=True)
    exponent = jnp.exp(scores - peak)
    attention_weights = (exponent / jnp.sum(exponent, axis=-1, keepdims=True)).astype(jnp.bfloat16)
    gathered = jnp.einsum(
        "whqk,wkhd->wqhd", attention_weights, values, preferred_element_type=jnp.float32
    )
    gathered = gathered.astype(jnp.bfloat16).reshape(count, span, features)
    return jnp.dot(gathered, w_proj, preferred_element_type=jnp.float32)


def attention_part(field, labels, gain_vector, w_qkv, w_proj):
    level_count, row_count, column_count, features = field.shape
    normed = layer_norm(field, gain_vector).astype(jnp.bfloat16)
    projected = window_attention(to_windows(normed), to_windows(labels), w_qkv, w_proj)
    return field.astype(jnp.float32) + from_windows(projected, level_count, row_count, column_count)


def feed_forward(field, gain_vector, w_up, w_down):
    normed = layer_norm(field, gain_vector).astype(jnp.bfloat16)
    hidden_units = jax.nn.gelu(jnp.dot(normed, w_up, preferred_element_type=jnp.float32)).astype(
        jnp.bfloat16
    )
    return (field + jnp.dot(hidden_units, w_down, preferred_element_type=jnp.float32)).astype(
        jnp.bfloat16
    )


def per_device(
    tokens, region, norm_gain1, qkv_weight, proj_weight, norm_gain2, up_weight, down_weight
):
    level_count, row_count, column_count, features = tokens.shape
    half_level = WLEV // 2
    half_row = WLAT // 2
    half_column = WLON // 2
    mixed_first = attention_part(tokens, region, norm_gain1[0], qkv_weight[0], proj_weight[0])
    first_out = feed_forward(mixed_first, norm_gain2[0], up_weight[0], down_weight[0])
    shifted = jnp.roll(first_out, -half_level, axis=0)
    label_field = jnp.roll(region.astype(jnp.bfloat16), -half_level, axis=0)
    below_field, below_labels = shifted_2(
        (shifted[:, :half_row], label_field[:, :half_row]), "lat", -1
    )
    shifted = jnp.concatenate([shifted[:, half_row:], below_field], axis=1)
    label_field = jnp.concatenate([label_field[:, half_row:], below_labels], axis=1)
    beside_field, beside_labels = shifted_2(
        (shifted[:, :, :half_column], label_field[:, :, :half_column]), "lon", -1
    )
    shifted = jnp.concatenate([shifted[:, :, half_column:], beside_field], axis=2)
    label_field = jnp.concatenate([label_field[:, :, half_column:], beside_labels], axis=2)
    level_index = jnp.arange(level_count, dtype=jnp.int32)[:, None, None]
    global_row = (
        lax.axis_index("lat") * row_count + jnp.arange(row_count, dtype=jnp.int32)[None, :, None]
    )
    wrapped_level = (level_index >= level_count - half_level).astype(jnp.int32)
    wrapped_row = (global_row >= row_count * lax.axis_size("lat") - half_row).astype(jnp.int32)
    labels_second = label_field.astype(jnp.int32) * 4 + wrapped_level * 2 + wrapped_row
    mixed_second = attention_part(
        shifted, labels_second, norm_gain1[1], qkv_weight[1], proj_weight[1]
    )
    keep_columns = column_count - half_column
    keep_rows = row_count - half_row
    finished = feed_forward(mixed_second, norm_gain2[1], up_weight[1], down_weight[1])
    left_part = shifted_2(finished[:, :, keep_columns:], "lon", 1)
    restored = jnp.concatenate([left_part, finished[:, :, :keep_columns]], axis=2)
    upper_part = shifted_2(restored[:, keep_rows:], "lat", 1)
    restored = jnp.concatenate([upper_part, restored[:, :keep_rows]], axis=1)
    return jnp.roll(restored, half_level, axis=0)


def solution(mesh):
    return jax.shard_map(
        per_device,
        mesh=mesh,
        in_specs=(P(None, "lat", "lon", None), P(None, "lat", "lon"), P(), P(), P(), P(), P(), P()),
        out_specs=P(None, "lat", "lon", None),
        check_vma=False,
    )
```

profile of v0, /device:TPU:0, one launch (start us, length us, event | category | flops | bytes accessed | tf_op | source)
XLA Modules:
  0.0 102.8 jit_solution(15368279036632336587)
XLA Ops:
  0.0 1.3 %convert_reduce_fusion.1 = f32[4,12,12]{2,1,0:T(8,128)S(1)} fusion(bf16[4,12,12,512]{3,0,2,1:T(4,128)(2,1)} %param.8), kind=kLoop, calls=%fused_computation.37 | loop fusion | flops 589248 | bytes 592128 | tf_op jit(solution)/shard_map/reduce_sum | solution.py:25
  1.4 1.5 %fusion.52 = f32[4,12,12]{2,1,0:T(8,128)S(1)} fusion(bf16[4,12,12,512]{3,0,2,1:T(4,128)(2,1)} %param.8, f32[4,12,12]{2,1,0:T(8,128)S(1)} %broadcast_multiply_fusion.3), kind=kLoop, calls=%fused_computation.60 | loop fusion | flops 1179072 | bytes 594432 | tf_op jit(solution)/shard_map/reduce_sum | solution.py:27
  2.9 0.8 fusion.120
  3.6 0.3 fusion.54
  4.0 0.6 copy.145
  4.6 0.2 reshape.272
  4.8 2.5 %convolution_convert_fusion.1 = bf16[4,144,1536]{2,1,0:T(8,128)(2,1)S(1)} fusion(bf16[2,512,1536]{2,1,0:T(8,128)(2,1)} %param.11, bf16[4,144,512]{2,0,1:T(4,128)(2,1)S(1)} %reshape.272), kind=kOutput, calls=%fused_computation.31 | convolution fusion | flops 906854400 | bytes 3932160 | tf_op jit(solution)/shard_map/dot_general | solution.py:53
  7.3 0.2 fusion.117
  7.5 0.5 copy.103
  8.0 1.3 %copy.104 = bf16[4,144,512]{1,2,0:T(8,128)(2,1)} copy(bf16[4,144,512]{2,1,0:T(8,128)(2,1)S(1)} %get-tuple-element.8) | data formatting | bytes 1179648 | tf_op jit(solution)/shard_map/reshape | solution.py:55
  9.5 1.3 %copy.102 = bf16[4,144,512]{1,2,0:T(8,128)(2,1)} copy(bf16[4,144,512]{2,1,0:T(8,128)(2,1)S(1)} %get-tuple-element.10) | data formatting | bytes 1179648 | tf_op jit(solution)/shard_map/reshape | solution.py:56
  10.8 4.0 %fusion.121 = (f32[4,8,144]{2,1,0:T(8,128)S(1)}, f32[4,8,144,144]{2,3,1,0:T(8,128)}) fusion(pred[4,144,144]{1,2,0:T(8,128)(4,1)S(1)} %broadcast_compare_fusion.1, bf16[4,144,8,64]{1,3,2,0:T(8,128)(2,1)S(1)} %bitcast.151, bf16[4,144,8,64]{1,3,2,0:T(8,128)(2,1)S(1)} %bitcast.152), kind=kOutput, calls=%fused_computation.152 | convolution fusion | flops 87589008 | bytes 3935232 | tf_op jit(solution)/shard_map/sub | solution.py:62
  14.8 3.2 %fusion.74 = bf16[4,144,8,64]{1,3,2,0:T(8,128)(2,1)S(1)} fusion(bf16[4,144,8,64]{1,3,2,0:T(8,128)(2,1)} %bitcast.154, f32[4,8,144,144]{2,3,1,0:T(8,128)} %get-tuple-element.22, f32[4,8,144]{2,1,0:T(8,128)S(1)} %get-tuple-element.21), kind=kOutput, calls=%fused_computation.83 | convolution fusion | flops 86556672 | bytes 3852288 | tf_op jit(solution)/shard_map/whqk,wkhd->wqhd/dot_general | solution.py:64
  18.0 0.8 copy.105
  18.9 0.8 reshape.293
  19.6 1.6 %convolution_bitcast_fusion.1 = f32[2,2,2,6,1,12,512]{6,5,3,1,2,0,4:T(8,128)S(1)} fusion(bf16[2,2,2,6,12,512]{5,4,3,2,1,0:T(8,128)(2,1)S(1)} %reshape.293, bf16[2,512,512]{2,1,0:T(8,128)(2,1)} %param.12), kind=kOutput, calls=%fused_computation.80 | convolution fusion | flops 301989888 | bytes 2293760 | tf_op jit(solution)/shard_map/dot_general | solution.py:68
  21.3 0.2 copy.106
  21.5 0.3 fusion.84
  21.8 0.5 multiply_reduce_fusion.1
  22.5 6.0 %add_convert_fusion = bf16[4,12,12,512]{3,2,1,0:T(8,128)(2,1)S(1)} fusion(bf16[2,2048,512]{2,1,0:T(8,128)(2,1)} %param.15, bf16[2,512,2048]{2,1,0:T(8,128)(2,1)} %param.14, f32[512]{0:T(512)S(1)} %bitcast.167, f32[4,12,12]{2,1,0:T(8,128)S(1)} %add_rsqrt_fusion.2, f32[4,12,12]{2,1,0:T(8,128)S(1)} %broadcast_multiply_fusion.2, ...), kind=kOutput, calls=%fused_computation.75 | convolution fusion | flops 2429485056 | bytes 9177088 | tf_op jit(solution)/shard_map/dot_general | solution.py:83
  28.6 2.4 %collective-permute-start = (bf16[4,3,12,512]{3,2,1,0:T(8,128)(2,1)S(1)}, bf16[4,3,12,512]{3,2,1,0:T(8,128)(2,1)S(1)}, u32[]{:S(2)}, u32[]{:S(2)}) collective-permute-start(bf16[4,3,12,512]{3,2,1,0:T(8,128)(2,1)S(1)} %pad_maximum_fusion.8), channel_id=1, source_target_pairs={{0,24},{8,0},{16,8},{24,16},{1,25},{9,1},{17,9},{25,17},{2,26},{10... | collective-permute-start | bytes 442376 | tf_op jit(solution)/shard_map/ppermute | solution.py:20
  31.1 0.7 collective-permute-start.2
  31.9 2.3 %collective-permute-done.2 = bf16[4,3,12]{2,0,1:T(4,128)(2,1)S(1)} collective-permute-done((bf16[4,3,12]{2,0,1:T(4,128)(2,1)S(1)}, bf16[4,3,12]{2,0,1:T(4,128)(2,1)S(1)}, u32[]{:S(2)}, u32[]{:S(2)}) %collective-permute-start.2) | collective-permute-done | bytes 320 | tf_op jit(solution)/shard_map/ppermute | solution.py:20
  34.3 4.6 %collective-permute-start.3 = (bf16[4,12,6]{2,0,1:T(4,128)(2,1)S(1)}, bf16[4,12,6]{2,0,1:T(4,128)(2,1)S(1)}, u32[]{:S(2)}, u32[]{:S(2)}) collective-permute-start(bf16[4,12,6]{2,0,1:T(4,128)(2,1)S(1)} %get-tuple-element.16), channel_id=1, source_target_pairs={{0,7},{1,0},{2,1},{3,2},{4,3},{5,4},{6,5},{7,6},{8,15},{9,8},{10,9... | collective-permute-start | bytes 1736 | tf_op jit(solution)/shard_map/ppermute | solution.py:20
  38.9 1.4 %collective-permute-done.3 = bf16[4,12,6]{2,0,1:T(4,128)(2,1)S(1)} collective-permute-done((bf16[4,12,6]{2,0,1:T(4,128)(2,1)S(1)}, bf16[4,12,6]{2,0,1:T(4,128)(2,1)S(1)}, u32[]{:S(2)}, u32[]{:S(2)}) %collective-permute-start.3) | collective-permute-done | bytes 608 | tf_op jit(solution)/shard_map/ppermute | solution.py:20
  40.5 5.2 %collective-permute-start.1 = (bf16[4,12,6,512]{3,2,1,0:T(8,128)(2,1)S(1)}, bf16[4,12,6,512]{3,2,1,0:T(8,128)(2,1)S(1)}, u32[]{:S(2)}, u32[]{:S(2)}) collective-permute-start(bf16[4,12,6,512]{3,2,1,0:T(8,128)(2,1)S(1)} %get-tuple-element.14), channel_id=1, source_target_pairs={{0,7},{1,0},{2,1},{3,2},{4,3},{5,4},{6,5},{7,6},{8,15},{9,8},{10,9... | collective-permute-start | bytes 884744 | tf_op jit(solution)/shard_map/ppermute | solution.py:20
  45.9 0.8 broadcast_compare_fusion
  46.7 7.5 %collective-permute-done.1 = bf16[4,12,6,512]{3,2,1,0:T(8,128)(2,1)S(1)} collective-permute-done((bf16[4,12,6,512]{3,2,1,0:T(8,128)(2,1)S(1)}, bf16[4,12,6,512]{3,2,1,0:T(8,128)(2,1)S(1)}, u32[]{:S(2)}, u32[]{:S(2)}) %collective-permute-start.1) | collective-permute-done | bytes 294944 | tf_op jit(solution)/shard_map/ppermute | solution.py:20
  54.3 0.4 convert_reduce_fusion
  54.7 0.5 fusion.59
  55.3 0.4 fusion.76
  55.8 2.5 %convolution_convert_fusion = bf16[4,144,1536]{2,1,0:T(8,128)(2,1)S(1)} fusion(bf16[4,144,512]{2,1,0:T(8,128)(2,1)S(1)} %reshape.294, bf16[2,512,1536]{2,1,0:T(8,128)(2,1)} %param.11), kind=kOutput, calls=%fused_computation.30 | convolution fusion | flops 906854400 | bytes 3932160 | tf_op jit(solution)/shard_map/dot_general | solution.py:53
  58.5 1.3 %copy.110 = bf16[4,144,512]{1,2,0:T(8,128)(2,1)} copy(bf16[4,144,512]{2,1,0:T(8,128)(2,1)S(1)} %get-tuple-element.6) | data formatting | bytes 1179648 | tf_op jit(solution)/shard_map/reshape | solution.py:54
  59.8 1.3 %copy.111 = bf16[4,144,512]{1,2,0:T(8,128)(2,1)} copy(bf16[4,144,512]{2,1,0:T(8,128)(2,1)S(1)} %get-tuple-element.5) | data formatting | bytes 1179648 | tf_op jit(solution)/shard_map/reshape | solution.py:55
  61.1 1.3 %copy.109 = bf16[4,144,512]{1,2,0:T(8,128)(2,1)} copy(bf16[4,144,512]{2,1,0:T(8,128)(2,1)S(1)} %get-tuple-element.7) | data formatting | bytes 1179648 | tf_op jit(solution)/shard_map/reshape | solution.py:56
  62.4 4.9 %fusion.122 = (f32[4,8,144]{2,1,0:T(8,128)S(1)}, f32[4,8,144,144]{2,3,1,0:T(8,128)}) fusion(pred[4,144,144]{1,2,0:T(8,128)(4,1)} %broadcast_compare_fusion, bf16[4,144,8,64]{1,3,2,0:T(8,128)(2,1)S(1)} %bitcast.153, bf16[4,144,8,64]{1,3,2,0:T(8,128)(2,1)S(1)} %bitcast.155), kind=kOutput, calls=%fused_computation.153 | convolution fusion | flops 87589008 | bytes 3935232 | tf_op jit(solution)/shard_map/sub | solution.py:62
  67.3 3.2 %fusion.75 = bf16[4,144,8,64]{1,3,2,0:T(8,128)(2,1)S(1)} fusion(bf16[4,144,8,64]{1,3,2,0:T(8,128)(2,1)} %bitcast.156, f32[4,8,144,144]{2,3,1,0:T(8,128)} %get-tuple-element.24, f32[4,8,144]{2,1,0:T(8,128)S(1)} %get-tuple-element.23), kind=kOutput, calls=%fused_computation.84 | convolution fusion | flops 86556672 | bytes 3852288 | tf_op jit(solution)/shard_map/whqk,wkhd->wqhd/dot_general | solution.py:64
  70.5 0.8 copy.112
  71.3 0.8 reshape.295
  72.1 1.8 %fusion.91 = (f32[2,2,2,6,12]{4,3,1,2,0:T(8,128)S(1)}, f32[2,2,2,6,1,12,512]{6,5,3,1,2,0,4:T(8,128)S(1)}) fusion(bf16[2,2,2,6,12,512]{5,4,3,2,1,0:T(8,128)(2,1)S(1)} %reshape.295, bf16[2,512,512]{2,1,0:T(8,128)(2,1)} %param.12, bf16[2,2,2,6,1,6,512]{6,5,3,2,1,0,4:T(8,128)(2,1)S(1)} %bitcast.145, bf16[2,2,2,6,1,6,512]{6,5,3,2,1,0,4:T(8,128)(2,1)S(1)} %bitcast.138), kind=kOutput, calls=%fused_computation.108 | convolution fusion | flops 304053696 | bytes 2885888 | tf_op jit(solution)/shard_map/dot_general | solution.py:68
  74.1 0.6 multiply_reduce_fusion
  74.7 0.5 multiply_convert_fusion
  75.2 0.9 copy.113
  76.2 6.1 %fusion.61 = bf16[4,12,12,512]{3,2,1,0:T(8,128)(2,1)S(1)} fusion(f32[4,12,12,512]{3,2,1,0:T(8,128)S(1)} %bitcast.150, bf16[4,12,6,512]{3,2,1,0:T(8,128)(2,1)S(1)} %collective-permute-done.1, bf16[4,12,6,512]{3,2,1,0:T(8,128)(2,1)S(1)} %get-tuple-element.13, bf16[2,2048,512]{2,1,0:T(8,128)(2,1)} %param.15, bf16[4,12,12,512]{3,2,1,0:T(8,128)(2,1)} %bitcast.157, ...), kind=kOutput, calls=%fused_computation.69 | convolution fusion | flops 2428600320 | bytes 7340032 | tf_op jit(solution)/shard_map/dot_general | solution.py:83
  82.5 13.6 %collective-permute-done.4 = bf16[4,12,6,512]{3,2,1,0:T(8,128)(2,1)S(1)} collective-permute-done((bf16[4,12,6,512]{3,2,1,0:T(8,128)(2,1)S(1)}, bf16[4,12,6,512]{3,2,1,0:T(8,128)(2,1)S(1)}, u32[]{:S(2)}, u32[]{:S(2)}) %collective-permute-start.4) | collective-permute-done | bytes 294944 | tf_op jit(solution)/shard_map/ppermute | solution.py:20
  96.2 5.1 %collective-permute-done.5 = bf16[4,3,12,512]{3,2,1,0:T(8,128)(2,1)S(1)} collective-permute-done((bf16[4,3,12,512]{3,2,1,0:T(8,128)(2,1)S(1)}, bf16[4,3,12,512]{3,2,1,0:T(8,128)(2,1)S(1)}, u32[]{:S(2)}, u32[]{:S(2)}) %collective-permute-start.5) | collective-permute-done | bytes 147488 | tf_op jit(solution)/shard_map/ppermute | solution.py:20
  101.3 0.2 fusion.77
  101.6 1.3 %copy.93 = bf16[4,12,12,512]{3,0,2,1:T(4,128)(2,1)} copy(bf16[4,12,12,512]{3,2,1,0:T(8,128)(2,1)S(1)} %fusion.77) | data formatting | bytes 1179648 | tf_op jit(solution)/shard_map/jit(_roll_static)/concatenate | solution.py:126
  (53 shorter events, 2.0 us)
Async XLA Ops:
  0.0 3.6 %copy-start = (bf16[4,12,12,512]{3,0,2,1:T(4,128)(2,1)S(1)}, bf16[4,12,12,512]{3,0,2,1:T(4,128)(2,1)}, u32[]{:S(2)}) copy-start(bf16[4,12,12,512]{3,0,2,1:T(4,128)(2,1)} %param.8) | copy-start | bytes 1769476
  7.5 1.8 %copy-start.4 = (s32[4,12,12]{2,0,1:T(4,128)S(1)}, s32[4,12,12]{2,0,1:T(4,128)}, u32[]{:S(2)}) copy-start(s32[4,12,12]{2,0,1:T(4,128)} %param.9) | copy-start | bytes 6916
  9.3 1.6 %copy-start.1 = (bf16[4,144,512]{1,2,0:T(8,128)(2,1)S(1)}, bf16[4,144,512]{1,2,0:T(8,128)(2,1)}, u32[]{:S(2)}) copy-start(bf16[4,144,512]{1,2,0:T(8,128)(2,1)} %copy.104) | copy-start | bytes 1769476
  21.8 0.7 copy-start.5
  28.6 11.7 %collective-permute-start = (bf16[4,3,12,512]{3,2,1,0:T(8,128)(2,1)S(1)}, bf16[4,3,12,512]{3,2,1,0:T(8,128)(2,1)S(1)}, u32[]{:S(2)}, u32[]{:S(2)}) collective-permute-start(bf16[4,3,12,512]{3,2,1,0:T(8,128)(2,1)S(1)} %pad_maximum_fusion.8), channel_id=1, source_target_pairs={{0,24},{8,0},{16,8},{24,16},{1,25},{9,1},{17,9},{25,17},{2,26},{10... | collective-permute-start | bytes 442376 | tf_op jit(solution)/shard_map/ppermute | solution.py:20
  31.1 3.2 %collective-permute-start.2 = (bf16[4,3,12]{2,0,1:T(4,128)(2,1)S(1)}, bf16[4,3,12]{2,0,1:T(4,128)(2,1)S(1)}, u32[]{:S(2)}, u32[]{:S(2)}) collective-permute-start(bf16[4,3,12]{2,0,1:T(4,128)(2,1)S(1)} %pad_maximum_fusion.10), channel_id=1, source_target_pairs={{0,24},{8,0},{16,8},{24,16},{1,25},{9,1},{17,9},{25,17},{2,26},{10... | collective-permute-start | bytes 872 | tf_op jit(solution)/shard_map/ppermute | solution.py:20
  34.3 6.0 %collective-permute-start.3 = (bf16[4,12,6]{2,0,1:T(4,128)(2,1)S(1)}, bf16[4,12,6]{2,0,1:T(4,128)(2,1)S(1)}, u32[]{:S(2)}, u32[]{:S(2)}) collective-permute-start(bf16[4,12,6]{2,0,1:T(4,128)(2,1)S(1)} %get-tuple-element.16), channel_id=1, source_target_pairs={{0,7},{1,0},{2,1},{3,2},{4,3},{5,4},{6,5},{7,6},{8,15},{9,8},{10,9... | collective-permute-start | bytes 1736 | tf_op jit(solution)/shard_map/ppermute | solution.py:20
  40.5 13.8 %collective-permute-start.1 = (bf16[4,12,6,512]{3,2,1,0:T(8,128)(2,1)S(1)}, bf16[4,12,6,512]{3,2,1,0:T(8,128)(2,1)S(1)}, u32[]{:S(2)}, u32[]{:S(2)}) collective-permute-start(bf16[4,12,6,512]{3,2,1,0:T(8,128)(2,1)S(1)} %get-tuple-element.14), channel_id=1, source_target_pairs={{0,7},{1,0},{2,1},{3,2},{4,3},{5,4},{6,5},{7,6},{8,15},{9,8},{10,9... | collective-permute-start | bytes 884744 | tf_op jit(solution)/shard_map/ppermute | solution.py:20
  59.8 2.6 %copy-start.2 = (bf16[4,144,512]{1,2,0:T(8,128)(2,1)S(1)}, bf16[4,144,512]{1,2,0:T(8,128)(2,1)}, u32[]{:S(2)}) copy-start(bf16[4,144,512]{1,2,0:T(8,128)(2,1)} %copy.110) | copy-start | bytes 1769476
  61.1 1.3 %copy-start.3 = (bf16[4,144,512]{1,2,0:T(8,128)(2,1)S(1)}, bf16[4,144,512]{1,2,0:T(8,128)(2,1)}, u32[]{:S(2)}) copy-start(bf16[4,144,512]{1,2,0:T(8,128)(2,1)} %copy.111) | copy-start | bytes 1769476
  82.5 13.6 %collective-permute-start.4 = (bf16[4,12,6,512]{3,2,1,0:T(8,128)(2,1)S(1)}, bf16[4,12,6,512]{3,2,1,0:T(8,128)(2,1)S(1)}, u32[]{:S(2)}, u32[]{:S(2)}) collective-permute-start(bf16[4,12,6,512]{3,2,1,0:T(8,128)(2,1)S(1)} %get-tuple-element.11), channel_id=1, source_target_pairs={{0,1},{1,2},{2,3},{3,4},{4,5},{5,6},{6,7},{7,0},{8,9},{9,10},{10,1... | collective-permute-start | bytes 884744 | tf_op jit(solution)/shard_map/ppermute | solution.py:20
  96.2 5.1 %collective-permute-start.5 = (bf16[4,3,12,512]{3,2,1,0:T(8,128)(2,1)S(1)}, bf16[4,3,12,512]{3,2,1,0:T(8,128)(2,1)S(1)}, u32[]{:S(2)}, u32[]{:S(2)}) collective-permute-start(bf16[4,3,12,512]{3,2,1,0:T(8,128)(2,1)S(1)} %pad_maximum_fusion.7), channel_id=1, source_target_pairs={{0,8},{8,16},{16,24},{24,0},{1,9},{9,17},{17,25},{25,1},{2,10},{10... | collective-permute-start | bytes 442376 | tf_op jit(solution)/shard_map/ppermute | solution.py:20
where the time goes:
time: 103 us
  matrix products  35.7 us (35%)
  waiting for transfers between devices  29.9 us (29%)
  local copies, waits for them, and re-layouts  15.5 us (15%)
  starting transfers between devices  13.1 us (13%)
  other arithmetic  8.23 us (8%)
    ppermute x6, waiting for transfers between devices, shifted_2(): return lax.ppermute(value, axis, pairs)  29.9 us
    ppermute x6, starting transfers between devices, shifted_2(): return lax.ppermute(value, axis, pairs)  13.1 us
    dot_general x2, matrix products, feed_forward(): jnp.dot(hidden_units, w_down, preferred_element_type=jnp.float32)  12.1 us
    sub x2, matrix products, window_attention(): exponent = jnp.exp(scores - peak)  8.88 us
    dot_general x2, matrix products, window_attention(): jnp.einsum('whqk,wkhd->wqhd', attention_weights, values, preferred_elemen...  6.32 us
    dot_general x2, matrix products, window_attention(): jnp.dot(normed, w_qkv, preferred_element_type=jnp.float32)  4.99 us
    dot_general x2, matrix products, window_attention(): return jnp.dot(gathered, w_proj, preferred_element_type=jnp.float32)  3.39 us
    another operation x4, local copies, waits for them, and re-layouts  3.25 us
  transfers between devices with their start and end apart: 6, of which 5 were waited for; matrix products, arithmetic and copies ran while one was open for 1% of the time, Pallas kernels for 0%

commit v1 on v0

v1 whole, which is shorter than its diff:
```python
import functools

import jax
import jax.numpy as jnp
from jax import lax
from jax.experimental import pallas as pl
from jax.experimental.pallas import tpu as pltpu
from jax.sharding import PartitionSpec as P

HEADS = 8
WLEV = 2
WLAT = 6
WLON = 12
EPSILON = 1e-05
FAR = -1e30
MESH = pl.DeviceIdType.MESH
F32 = jnp.float32
BF16 = jnp.bfloat16


def normed(field, gain):
    mean = jnp.mean(field, axis=-1, keepdims=True)
    centered = field - mean
    variance = jnp.mean(centered * centered, axis=-1, keepdims=True)
    return (centered * lax.rsqrt(variance + EPSILON) * gain).astype(BF16)


def gelu(x):
    inner = x * (0.7978845608028654 + 0.035677408136300125 * (x * x))
    half = 0.5 * x
    return half + half * jnp.tanh(inner)


def dot(a, b):
    return jnp.dot(a, b, preferred_element_type=F32)


def dot_t(a, b):
    return lax.dot_general(a, b, (((1,), (1,)), ((), ())), preferred_element_type=F32)


def kernel(
    x_ref, e_ref, g1_ref, g2_ref, wqkv_hbm, wproj_hbm, wup_hbm, wdown_hbm, out_ref,
    own, shift, back, eshift, xin, qkv, heads, bias,
    wqkv, wproj, wup, wdown, wsem, fsend, frecv, bsend, brecv, esend, erecv,
):
    lat_count, lon_count = lax.axis_size("lat"), lax.axis_size("lon")
    lat, lon = lax.axis_index("lat"), lax.axis_index("lon")
    up = lax.rem(lat + lat_count - 1, lat_count)
    down = lax.rem(lat + 1, lat_count)
    left = lax.rem(lon + lon_count - 1, lon_count)
    right = lax.rem(lon + 1, lon_count)
    before = {"left": (lat, left), "up": (up, lon), "corner": (up, left)}
    after = {"left": (lat, right), "up": (down, lon), "corner": (down, right)}

    weights = []
    for block in range(2):
        for at, (source, target) in enumerate(
            ((wqkv_hbm, wqkv), (wproj_hbm, wproj), (wup_hbm, wup), (wdown_hbm, wdown))
        ):
            copy = pltpu.make_async_copy(
                source.at[block], target.at[block], wsem.at[block * 4 + at]
            )
            copy.start()
            weights.append(copy)

    barrier = pltpu.get_barrier_semaphore()
    for device in list(before.values()) + list(after.values()):
        pl.semaphore_signal(barrier, inc=1, device_id=device, device_id_type=MESH)
    pl.semaphore_wait(barrier, 6)

    moves = (
        (2, 0, 1, "left"),
        (4, 0, 3, "left"),
        (6, 1, 1, "left"),
        (1, 1, 2, "up"),
        (0, 1, 3, "corner"),
    )

    def label_copy(at):
        atom, window, place, towards = moves[at]
        return pltpu.make_async_remote_copy(
            e_ref.at[atom], eshift.at[window, place], esend.at[at], erecv.at[at],
            device_id=before[towards], device_id_type=MESH,
        )

    def forward_copy(at):
        atom, window, place, towards = moves[at]
        return pltpu.make_async_remote_copy(
            own.at[atom], shift.at[window, place], fsend.at[at], frecv.at[at],
            device_id=before[towards], device_id_type=MESH,
        )

    def backward_copy(at):
        atom, window, place, towards = moves[at]
        return pltpu.make_async_remote_copy(
            back.at[window, place], out_ref.at[atom], bsend.at[at], brecv.at[at],
            device_id=after[towards], device_id_type=MESH,
        )

    for at in range(5):
        label_copy(at).start()

    span, features = xin.shape
    atom_size = span // 4
    pair = 128
    lane = lax.broadcasted_iota(jnp.int32, (1, pair), 1)
    low = lane < 64
    scale = 64 ** -0.5
    head_masks = (
        jnp.where(low, scale, 0.0).astype(BF16),
        jnp.where(low, 0.0, scale).astype(BF16),
    )

    def set_bias(marks, block):
        half = low if block == 0 else jnp.logical_not(low)
        query = (marks * jnp.where(half, FAR, 0.0)).astype(BF16)
        key = (1.0 - marks).astype(BF16)
        bias[...] = dot_t(query, key)

    def unit(x, block, waits):
        if waits:
            weights[block * 4].wait()
        qkv[...] = dot(normed(x, g1_ref[block : block + 1, :]), wqkv[block]).astype(BF16)
        ones = jnp.ones((span, pair), BF16)
        for at in range(features // pair):
            cols = slice(at * pair, (at + 1) * pair)
            query = qkv[:, cols]
            key = qkv[:, features + at * pair : features + (at + 1) * pair]
            value = qkv[:, 2 * features + at * pair : 2 * features + (at + 1) * pair]
            value = jnp.concatenate([value, ones], axis=1)
            parts = []
            for mask in head_masks:
                scores = dot_t(query * mask, key) + bias[...]
                peak = jnp.max(scores, axis=-1, keepdims=True)
                weight = jnp.exp(scores - peak).astype(BF16)
                total = dot(weight, value)
                parts.append(total[:, :pair] / total[:, pair:])
            heads[:, cols] = jnp.where(low, parts[0], parts[1]).astype(BF16)
        if waits:
            weights[block * 4 + 1].wait()
        h = x + dot(heads[...], wproj[block])
        n2 = normed(h, g2_ref[block : block + 1, :])
        if waits:
            weights[block * 4 + 2].wait()
            weights[block * 4 + 3].wait()
        hidden = wup.shape[2]
        step = 512
        for at in range(hidden // step):
            cols = slice(at * step, (at + 1) * step)
            inner = gelu(dot(n2, wup[block, :, cols])).astype(BF16)
            h = h + dot(inner, wdown[block, cols, :])
        return h

    def rows(ref, first):
        return jnp.concatenate([ref[first + at].astype(F32) for at in range(4)], axis=0)

    for u in range(2):
        set_bias(rows(e_ref, 4 * u), 0)
        h = unit(rows(x_ref, 4 * u), 0, u == 0)
        for at in range(4):
            own[4 * u + at] = h[at * atom_size : (at + 1) * atom_size].astype(BF16)
        for at, move in enumerate(moves):
            if move[0] // 4 == u:
                forward_copy(at).start()

    local = {(0, 0): 3, (0, 2): 5, (1, 0): 7}
    arrivals = {(move[1], move[2]): at for at, move in enumerate(moves)}
    for w in range(2):
        for place in range(4):
            if (w, place) in arrivals:
                label_copy(arrivals[w, place]).wait_recv()
                forward_copy(arrivals[w, place]).wait_recv()
        marks = jnp.concatenate(
            [
                (e_ref[local[w, place]] if (w, place) in local else eshift[w, place]).astype(F32)
                for place in range(4)
            ],
            axis=0,
        )
        set_bias(marks, 1)
        x = jnp.concatenate(
            [
                (own[local[w, place]] if (w, place) in local else shift[w, place]).astype(F32)
                for place in range(4)
            ],
            axis=0,
        )
        h = unit(x, 1, w == 0)
        for place in range(4):
            piece = h[place * atom_size : (place + 1) * atom_size].astype(BF16)
            if (w, place) in local:
                out_ref[local[w, place]] = piece
            else:
                back[w, place] = piece
        for at, move in enumerate(moves):
            if move[1] == w:
                backward_copy(at).start()
    for at in range(5):
        backward_copy(at).wait_recv()
    for at in range(5):
        label_copy(at).wait_send()
        forward_copy(at).wait_send()
        backward_copy(at).wait_send()


def to_atoms(field):
    levels, row_count, column_count = field.shape[:3]
    trailing = tuple(field.shape[3:])
    half_row, half_column = WLAT // 2, WLON // 2
    shaped = field.reshape(
        (levels, row_count // half_row, half_row, column_count // half_column, half_column)
        + trailing
    )
    order = (1, 3, 0, 2, 4) + tuple(range(5, 5 + len(trailing)))
    return jnp.transpose(shaped, order).reshape(
        (-1, levels * half_row * half_column) + trailing
    )


def from_atoms(atoms, levels, row_count, column_count):
    trailing = tuple(atoms.shape[2:])
    half_row, half_column = WLAT // 2, WLON // 2
    shaped = atoms.reshape(
        (row_count // half_row, column_count // half_column, levels, half_row, half_column)
        + trailing
    )
    order = (2, 0, 3, 1, 4) + tuple(range(5, 5 + len(trailing)))
    return jnp.transpose(shaped, order).reshape((levels, row_count, column_count) + trailing)


def per_device(
    tokens, region, norm_gain1, qkv_weight, proj_weight, norm_gain2, up_weight, down_weight
):
    levels, row_count, column_count, features = tokens.shape
    hidden = up_weight.shape[2]
    x = to_atoms(tokens)
    atoms, size, _ = x.shape
    span = 4 * size

    level = jnp.arange(levels, dtype=jnp.int32)[:, None, None]
    row = (lax.axis_index("lat") * row_count + jnp.arange(row_count, dtype=jnp.int32))[None, :, None]
    pair_first = level // WLEV
    rolled_level = (level + levels - WLEV // 2) % levels
    wrapped_level = (rolled_level >= levels - WLEV // 2).astype(jnp.int32)
    wrapped_row = (row < WLAT // 2).astype(jnp.int32)
    first_class = region * 2 + pair_first
    second_class = ((region * 2 + rolled_level // WLEV) * 2 + wrapped_level) * 2 + wrapped_row
    classes = jnp.stack([first_class, second_class + 64], axis=-1)
    classes = to_atoms(classes)
    lane = jnp.arange(128, dtype=jnp.int32)
    marks = (
        (classes[:, :, :1] == lane) | (classes[:, :, 1:] == lane)
    ).astype(BF16)

    vmem = pl.BlockSpec(memory_space=pltpu.VMEM)
    hbm = pl.BlockSpec(memory_space=pl.ANY)
    out = pl.pallas_call(
        kernel,
        out_shape=jax.ShapeDtypeStruct((atoms, size, features), BF16),
        in_specs=[vmem] * 4 + [hbm] * 4,
        out_specs=vmem,
        scratch_shapes=[
            pltpu.VMEM((atoms, size, features), BF16),
            pltpu.VMEM((2, 4, size, features), BF16),
            pltpu.VMEM((2, 4, size, features), BF16),
            pltpu.VMEM((2, 4, size, 128), BF16),
            pltpu.VMEM((span, features), F32),
            pltpu.VMEM((span, 3 * features), BF16),
            pltpu.VMEM((span, features), BF16),
            pltpu.VMEM((span, span), F32),
            pltpu.VMEM(qkv_weight.shape, BF16),
            pltpu.VMEM(proj_weight.shape, BF16),
            pltpu.VMEM(up_weight.shape, BF16),
            pltpu.VMEM(down_weight.shape, BF16),
            pltpu.SemaphoreType.DMA((8,)),
            pltpu.SemaphoreType.DMA((5,)),
            pltpu.SemaphoreType.DMA((5,)),
            pltpu.SemaphoreType.DMA((5,)),
            pltpu.SemaphoreType.DMA((5,)),
            pltpu.SemaphoreType.DMA((5,)),
            pltpu.SemaphoreType.DMA((5,)),
        ],
        compiler_params=pltpu.CompilerParams(
            collective_id=0, has_side_effects=True, vmem_limit_bytes=50 * 1024 * 1024
        ),
    )(x, marks, norm_gain1, norm_gain2, qkv_weight, proj_weight, up_weight, down_weight)
    return from_atoms(out, levels, row_count, column_count)


def solution(mesh):
    return jax.shard_map(
        per_device,
        mesh=mesh,
        in_specs=(P(None, "lat", "lon", None), P(None, "lat", "lon"), P(), P(), P(), P(), P(), P()),
        out_specs=P(None, "lat", "lon", None),
        check_vma=False,
    )
```

time: 103 us -> 44.8 us (0.43)
  Pallas kernels: 0 us -> 39.1 us
  matrix products: 35.7 us -> 0 us
  waiting for transfers between devices: 29.9 us -> 0 us
  starting transfers between devices: 13.1 us -> 0 us
  local copies, waits for them, and re-layouts: 15.5 us -> 4.03 us
  other arithmetic: 8.23 us -> 1.19 us
    pallas_call x0 -> x1, Pallas kernels: none -> 39.1 us  [per_device(): pl.pallas_call(kernel, out_shape=jax.ShapeDtypeStruct((atoms, size, featu...]
    ppermute x6 -> x0, waiting for transfers between devices: 29.9 us -> none  [shifted_2(): return lax.ppermute(value, axis, pairs)]
    dot_general x8 -> x0, matrix products: 26.8 us -> none  [the longest x2 12.1 us: feed_forward(): jnp.dot(hidden_units, w_down, preferred_element_type=jnp.float32)]
    ppermute x6 -> x0, starting transfers between devices: 13.1 us -> none  [shifted_2(): return lax.ppermute(value, axis, pairs)]
    sub x2 -> x0, matrix products: 8.88 us -> none  [window_attention(): exponent = jnp.exp(scores - peak)]
    reshape x11 -> x5, local copies, waits for them, and re-layouts: 8.15 us -> 2.33 us  [the longest x1 1.57 us: to_atoms(): field.reshape((levels, row_count // half_row, half_row, column_count // h...]
    reduce_sum x7 -> x0, other arithmetic: 5.16 us -> none  [the longest x4 3.11 us: layer_norm(): variance = jnp.mean(centered * centered, axis=-1, keepdims=True)]
    another operation x4, local copies, waits for them, and re-layouts: 3.25 us -> 0.24 us  [per_device(): classes = jnp.stack([first_class, second_class + 64], axis=-1)]
  transfers between devices with their start and end apart: 6 -> 0, of which waited for: 5 -> 0; matrix products, arithmetic and copies ran while one was open for 1% -> 0% of each run, Pallas kernels for 0% -> 0%
where the time goes in v1:
time: 44.8 us; the launch traced here: 44.5 us
  Pallas kernels  39.1 us (87%)
  local copies, waits for them, and re-layouts  4.03 us (9%)
  other arithmetic  1.19 us (3%)
    pallas_call x1, Pallas kernels, per_device(): pl.pallas_call(kernel, out_shape=jax.ShapeDtypeStruct((atoms, size, featu...  39.1 us
    reshape x1, local copies, waits for them, and re-layouts, to_atoms(): field.reshape((levels, row_count // half_row, half_row, column_count // h...  1.57 us
    transpose x1, local copies, waits for them, and re-layouts, from_atoms(): jnp.transpose(shaped, order)  1.27 us
    add x1, other arithmetic, per_device(): first_class = region * 2 + pair_first  0.91 us

profile of v1, /device:TPU:0, one launch (start us, length us, event | category | flops | bytes accessed | tf_op | source)
XLA Modules:
  0.0 44.5 jit_solution(6615184479291466903)
XLA Ops:
  0.0 0.0 copy-start.2
  0.0 0.0 copy-start
  0.0 0.0 copy-start.1
  0.0 0.9 %multiply_add_fusion = (s32[4,12,12]{2,0,1:T(4,128)S(1)}, s32[4,12,12]{2,0,1:T(4,128)S(1)}) fusion(s32[4,12,12]{2,0,1:T(4,128)} %param.9, s32[4]{0:T(128)S(1)} %get-tuple-element.10, s32[12]{0:T(128)S(1)} %compare_convert_fusion, s32[4]{0:T(128)S(1)} %compare_convert_fusion.1, s32[4]{0:T(128)S(1)} %get-tuple-element.9), kind=kLoop, calls=%fused_computation.7 | loop fusion | flops 4608 | bytes 7008 | tf_op jit(solution)/shard_map/add | solution.py:247
  1.0 0.1 stack.9
  1.1 0.1 stack.10
  1.3 0.1 reshape.128
  1.4 0.2 fusion.1.e_ref
  1.6 1.6 %copy.24 = bf16[4,4,3,2,6,512]{5,3,1,4,2,0:T(2,128)(2,1)S(1)} copy(bf16[4,4,3,2,6,512]{5,0,4,3,2,1:T(4,128)(2,1)} %bitcast.24) | data formatting | bytes 1179648 | tf_op jit(solution)/shard_map/reshape | solution.py:211
  3.2 0.2 reshape.127
  3.4 0.2 copy.20.x_ref
  3.6 0.0 copy-done.2
  3.6 0.0 copy-done
  3.6 0.0 copy-done.1
  3.7 39.1 %shard_map.82 = bf16[8,72,512]{2,1,0:T(8,128)(2,1)S(1)} custom-call(bf16[8,72,512]{2,1,0:T(8,128)(2,1)S(1)} %copy.20.x_ref, bf16[8,72,128]{2,1,0:T(8,128)(2,1)S(1)} %fusion.1.e_ref, f32[2,512]{1,0:T(2,128)S(1)} %copy-done.1, f32[2,512]{1,0:T(2,128)S(1)} %copy-done.2, bf16[2,512,1536]{2,1,0:T(8,128)(2,1)} %wqkv_hbm.1, bf16[2,512,512]{2,1,0:T(8,128)(2,1)S(1)} %copy-done, ...), custom_call_target="tpu_custom_call" | custom-call | tf_op jit(solution)/shard_map/pallas_call | solution.py:258
  42.8 0.2 copy.21
  43.0 0.2 reshape.129
  43.2 1.3 %copy.22 = bf16[4,4,3,2,6,512]{5,0,4,3,2,1:T(4,128)(2,1)} copy(bf16[4,4,3,2,6,512]{5,3,1,4,2,0:T(2,128)(2,1)S(1)} %bitcast.22) | data formatting | bytes 1179648 | tf_op jit(solution)/shard_map/transpose | solution.py:229
  (7 shorter events, 0.1 us)
Async XLA Ops:
  0.0 3.6 %copy-start.2 = (f32[2,512]{1,0:T(2,128)S(1)}, f32[2,512]{1,0:T(2,128)}, u32[]{:S(2)}) copy-start(f32[2,512]{1,0:T(2,128)} %g2_ref.1) | copy-start | bytes 12292
  0.0 3.6 %copy-start = (bf16[2,512,512]{2,1,0:T(8,128)(2,1)S(1)}, bf16[2,512,512]{2,1,0:T(8,128)(2,1)}, u32[]{:S(2)}) copy-start(bf16[2,512,512]{2,1,0:T(8,128)(2,1)} %wproj_hbm.1) | copy-start | bytes 3145732
  0.0 3.6 %copy-start.1 = (f32[2,512]{1,0:T(2,128)S(1)}, f32[2,512]{1,0:T(2,128)}, u32[]{:S(2)}) copy-start(f32[2,512]{1,0:T(2,128)} %g1_ref.1) | copy-start | bytes 12292

commit v2 on v1

--- a/solution.py
+++ b/solution.py
@@ -41,7 +41,7 @@
 
 def kernel(
     x_ref, e_ref, g1_ref, g2_ref, wqkv_hbm, wproj_hbm, wup_hbm, wdown_hbm, out_ref,
-    own, shift, back, eshift, xin, qkv, heads, bias,
+    own, shift, back, eshift, xs, qkv, heads, bias,
     wqkv, wproj, wup, wdown, wsem, fsend, frecv, bsend, brecv, esend, erecv,
 ):
     lat_count, lon_count = lax.axis_size("lat"), lax.axis_size("lon")
@@ -53,29 +53,29 @@
     before = {"left": (lat, left), "up": (up, lon), "corner": (up, left)}
     after = {"left": (lat, right), "up": (down, lon), "corner": (down, right)}
 
-    weights = []
-    for block in range(2):
+    weights = [
+        pltpu.make_async_copy(source.at[block], target.at[block], wsem.at[block * 4 + at])
+        for block in range(2)
         for at, (source, target) in enumerate(
             ((wqkv_hbm, wqkv), (wproj_hbm, wproj), (wup_hbm, wup), (wdown_hbm, wdown))
-        ):
-            copy = pltpu.make_async_copy(
-                source.at[block], target.at[block], wsem.at[block * 4 + at]
-            )
-            copy.start()
-            weights.append(copy)
+        )
+    ]
+    weights[0].start()
+    weights[1].start()
 
     barrier = pltpu.get_barrier_semaphore()
     for device in list(before.values()) + list(after.values()):
         pl.semaphore_signal(barrier, inc=1, device_id=device, device_id_type=MESH)
-    pl.semaphore_wait(barrier, 6)
 
     moves = (
-        (2, 0, 1, "left"),
-        (4, 0, 3, "left"),
-        (6, 1, 1, "left"),
+        (2, 0, 0, "left"),
+        (0, 1, 1, "corner"),
+        (4, 0, 1, "left"),
+        (6, 1, 0, "left"),
         (1, 1, 2, "up"),
-        (0, 1, 3, "corner"),
-    )
+    )
+    local = {(0, 2): 3, (0, 3): 5, (1, 3): 7}
+    arrivals = {(move[1], move[2]): at for at, move in enumerate(moves)}
 
     def label_copy(at):
         atom, window, place, towards = moves[at]
@@ -98,11 +98,9 @@
             device_id=after[towards], device_id_type=MESH,
         )
 
-    for at in range(5):
-        label_copy(at).start()
-
-    span, features = xin.shape
+    span, features = xs.shape[1:]
     atom_size = span // 4
+    part_size = span // 2
     pair = 128
     lane = lax.broadcasted_iota(jnp.int32, (1, pair), 1)
     low = lane < 64
@@ -112,90 +110,112 @@
         jnp.where(low, 0.0, scale).astype(BF16),
     )
 
-    def set_bias(marks, block):
+    def prepare(block, at, pieces, marks):
+        index = 2 * block + at
+        marks = jnp.concatenate([piece.astype(F32) for piece in marks], axis=0)
         half = low if block == 0 else jnp.logical_not(low)
         query = (marks * jnp.where(half, FAR, 0.0)).astype(BF16)
-        key = (1.0 - marks).astype(BF16)
-        bias[...] = dot_t(query, key)
-
-    def unit(x, block, waits):
-        if waits:
+        bias[index] = dot_t(query, (1.0 - marks).astype(BF16))
+        x = jnp.concatenate([piece.astype(F32) for piece in pieces], axis=0)
+        xs[index] = x
+        n1 = normed(x, g1_ref[block : block + 1, :])
+        if at == 0:
             weights[block * 4].wait()
-        qkv[...] = dot(normed(x, g1_ref[block : block + 1, :]), wqkv[block]).astype(BF16)
+        qkv[index] = dot(n1, wqkv[block]).astype(BF16)
+
+    def part(block, at, which, first):
+        index = 2 * block + at
+        rows = slice(which * part_size, (which + 1) * part_size)
         ones = jnp.ones((span, pair), BF16)
-        for at in range(features // pair):
-            cols = slice(at * pair, (at + 1) * pair)
-            query = qkv[:, cols]
-            key = qkv[:, features + at * pair : features + (at + 1) * pair]
-            value = qkv[:, 2 * features + at * pair : 2 * features + (at + 1) * pair]
+        offset = bias[index, rows, :]
+        offset = jnp.concatenate([offset, offset], axis=0)
+        for column in range(0, features, pair):
+            query = qkv[index, rows, column : column + pair]
+            key = qkv[index, :, features + column : features + column + pair]
+            value = qkv[index, :, 2 * features + column : 2 * features + column + pair]
             value = jnp.concatenate([value, ones], axis=1)
-            parts = []
-            for mask in head_masks:
-                scores = dot_t(query * mask, key) + bias[...]
-                peak = jnp.max(scores, axis=-1, keepdims=True)
-                weight = jnp.exp(scores - peak).astype(BF16)
-                total = dot(weight, value)
-                parts.append(total[:, :pair] / total[:, pair:])
-            heads[:, cols] = jnp.where(low, parts[0], parts[1]).astype(BF16)
-        if waits:
+            query = jnp.concatenate([query * head_masks[0], query * head_masks[1]], axis=0)
+            scores = dot_t(query, key) + offset
+            peak = jnp.max(scores, axis=-1, keepdims=True)
+            weight = jnp.exp(scores - peak).astype(BF16)
+            total = dot(weight, value)
+            total = total[:, :pair] / total[:, pair:]
+            heads[index, rows, column : column + pair] = jnp.where(
+                low, total[:part_size], total[part_size:]
+            ).astype(BF16)
+        if first:
             weights[block * 4 + 1].wait()
-        h = x + dot(heads[...], wproj[block])
+        h = xs[index, rows, :] + dot(heads[index, rows, :], wproj[block])
         n2 = normed(h, g2_ref[block : block + 1, :])
-        if waits:
+        if first:
             weights[block * 4 + 2].wait()
             weights[block * 4 + 3].wait()
         hidden = wup.shape[2]
         step = 512
-        for at in range(hidden // step):
-            cols = slice(at * step, (at + 1) * step)
-            inner = gelu(dot(n2, wup[block, :, cols])).astype(BF16)
-            h = h + dot(inner, wdown[block, cols, :])
-        return h
-
-    def rows(ref, first):
-        return jnp.concatenate([ref[first + at].astype(F32) for at in range(4)], axis=0)
-
-    for u in range(2):
-        set_bias(rows(e_ref, 4 * u), 0)
-        h = unit(rows(x_ref, 4 * u), 0, u == 0)
-        for at in range(4):
-            own[4 * u + at] = h[at * atom_size : (at + 1) * atom_size].astype(BF16)
-        for at, move in enumerate(moves):
-            if move[0] // 4 == u:
-                forward_copy(at).start()
-
-    local = {(0, 0): 3, (0, 2): 5, (1, 0): 7}
-    arrivals = {(move[1], move[2]): at for at, move in enumerate(moves)}
-    for w in range(2):
+        for column in range(0, hidden, step):
+            inner = gelu(dot(n2, wup[block, :, column : column + step])).astype(BF16)
+            h = h + dot(inner, wdown[block, column : column + step, :])
+        return h[:atom_size].astype(BF16), h[atom_size:].astype(BF16)
+
+    def prepare_first(u):
+        atoms = (4 * u, 4 * u + 2, 4 * u + 1, 4 * u + 3)
+        prepare(0, u, [x_ref[a] for a in atoms], [e_ref[a] for a in atoms])
+
+    def part_first(u, which, first=False):
+        own[4 * u + which], own[4 * u + 2 + which] = part(0, u, which, first)
+
+    prepare_first(0)
+    weights[2].start()
+    weights[3].start()
+    part_first(0, 0, True)
+    pl.semaphore_wait(barrier, 6)
+    for at in range(5):
+        label_copy(at).start()
+    forward_copy(0).start()
+    forward_copy(1).start()
+    for at in range(4, 8):
+        weights[at].start()
+    prepare_first(1)
+    part_first(1, 0)
+    forward_copy(2).start()
+    forward_copy(3).start()
+    part_first(0, 1)
+    forward_copy(4).start()
+    part_first(1, 1)
+
+    def prepare_second(w):
+        pieces, marks = [], []
         for place in range(4):
             if (w, place) in arrivals:
                 label_copy(arrivals[w, place]).wait_recv()
                 forward_copy(arrivals[w, place]).wait_recv()
-        marks = jnp.concatenate(
-            [
-                (e_ref[local[w, place]] if (w, place) in local else eshift[w, place]).astype(F32)
-                for place in range(4)
-            ],
-            axis=0,
-        )
-        set_bias(marks, 1)
-        x = jnp.concatenate(
-            [
-                (own[local[w, place]] if (w, place) in local else shift[w, place]).astype(F32)
-                for place in range(4)
-            ],
-            axis=0,
-        )
-        h = unit(x, 1, w == 0)
         for place in range(4):
-            piece = h[place * atom_size : (place + 1) * atom_size].astype(BF16)
+            if (w, place) in arrivals:
+                pieces.append(shift[w, place])
+                marks.append(eshift[w, place])
+            else:
+                pieces.append(own[local[w, place]])
+                marks.append(e_ref[local[w, place]])
+        prepare(1, w, pieces, marks)
+
+    def part_second(w, which, first=False):
+        results = part(1, w, which, first)
+        for at in range(2):
+            place = 2 * which + at
             if (w, place) in local:
-                out_ref[local[w, place]] = piece
+                out_ref[local[w, place]] = results[at]
             else:
-                back[w, place] = piece
-        for at, move in enumerate(moves):
-            if move[1] == w:
-                backward_copy(at).start()
+                back[w, place] = results[at]
+        for at in range(2):
+            if (w, 2 * which + at) in arrivals:
+                backward_copy(arrivals[w, 2 * which + at]).start()
+
+    prepare_second(0)
+    part_second(0, 0, True)
+    prepare_second(1)
+    part_second(1, 0)
+    part_second(1, 1)
+    part_second(0, 1)
     for at in range(5):
         backward_copy(at).wait_recv()
     for at in range(5):
@@ -265,10 +285,10 @@
             pltpu.VMEM((2, 4, size, features), BF16),
             pltpu.VMEM((2, 4, size, features), BF16),
             pltpu.VMEM((2, 4, size, 128), BF16),
-            pltpu.VMEM((span, features), F32),
-            pltpu.VMEM((span, 3 * features), BF16),
-            pltpu.VMEM((span, features), BF16),
-            pltpu.VMEM((span, span), F32),
+            pltpu.VMEM((4, span, features), F32),
+            pltpu.VMEM((4, span, 3 * features), BF16),
+            pltpu.VMEM((4, span, features), BF16),
+            pltpu.VMEM((4, span, span), F32),
             pltpu.VMEM(qkv_weight.shape, BF16),
             pltpu.VMEM(proj_weight.shape, BF16),
             pltpu.VMEM(up_weight.shape, BF16),

time: 44.8 us -> 38.3 us (0.85)
  Pallas kernels: 39.1 us -> 32.7 us
    pallas_call x1, Pallas kernels: 39.1 us -> 32.7 us  [per_device(): pl.pallas_call(kernel, out_shape=jax.ShapeDtypeStruct((atoms, size, featu...]
where the time goes in v2:
time: 38.3 us; the launch traced here: 38.1 us
  Pallas kernels  32.7 us (85%)
  local copies, waits for them, and re-layouts  4.03 us (11%)
  other arithmetic  1.19 us (3%)
    pallas_call x1, Pallas kernels, per_device(): pl.pallas_call(kernel, out_shape=jax.ShapeDtypeStruct((atoms, size, featu...  32.7 us
    reshape x1, local copies, waits for them, and re-layouts, to_atoms(): field.reshape((levels, row_count // half_row, half_row, column_count // h...  1.57 us
    transpose x1, local copies, waits for them, and re-layouts, from_atoms(): jnp.transpose(shaped, order)  1.27 us
    add x1, other arithmetic, per_device(): first_class = region * 2 + pair_first  0.91 us

profile of v2, /device:TPU:0, one launch (start us, length us, event | category | flops | bytes accessed | tf_op | source)
XLA Modules:
  0.0 38.1 jit_solution(13606005750275088441)
XLA Ops:
  0.0 0.0 copy-start.2
  0.0 0.0 copy-start
  0.0 0.0 copy-start.1
  0.0 0.9 %multiply_add_fusion = (s32[4,12,12]{2,0,1:T(4,128)S(1)}, s32[4,12,12]{2,0,1:T(4,128)S(1)}) fusion(s32[4,12,12]{2,0,1:T(4,128)} %param.9, s32[4]{0:T(128)S(1)} %get-tuple-element.10, s32[12]{0:T(128)S(1)} %compare_convert_fusion, s32[4]{0:T(128)S(1)} %compare_convert_fusion.1, s32[4]{0:T(128)S(1)} %get-tuple-element.9), kind=kLoop, calls=%fused_computation.7 | loop fusion | flops 4608 | bytes 7008 | tf_op jit(solution)/shard_map/add | solution.py:267
  1.0 0.1 stack.9
  1.1 0.1 stack.10
  1.3 0.1 reshape.128
  1.4 0.2 fusion.1.e_ref
  1.6 1.6 %copy.24 = bf16[4,4,3,2,6,512]{5,3,1,4,2,0:T(2,128)(2,1)S(1)} copy(bf16[4,4,3,2,6,512]{5,0,4,3,2,1:T(4,128)(2,1)} %bitcast.24) | data formatting | bytes 1179648 | tf_op jit(solution)/shard_map/reshape | solution.py:231
  3.2 0.2 reshape.127
  3.4 0.2 copy.20.x_ref
  3.6 0.0 copy-done.2
  3.6 0.0 copy-done
  3.6 0.0 copy-done.1
  3.7 32.7 %shard_map.82 = bf16[8,72,512]{2,1,0:T(8,128)(2,1)S(1)} custom-call(bf16[8,72,512]{2,1,0:T(8,128)(2,1)S(1)} %copy.20.x_ref, bf16[8,72,128]{2,1,0:T(8,128)(2,1)S(1)} %fusion.1.e_ref, f32[2,512]{1,0:T(2,128)S(1)} %copy-done.1, f32[2,512]{1,0:T(2,128)S(1)} %copy-done.2, bf16[2,512,1536]{2,1,0:T(8,128)(2,1)} %wqkv_hbm.1, bf16[2,512,512]{2,1,0:T(8,128)(2,1)S(1)} %copy-done, ...), custom_call_target="tpu_custom_call" | custom-call | tf_op jit(solution)/shard_map/pallas_call | solution.py:278
  36.4 0.2 copy.21
  36.6 0.2 reshape.129
  36.8 1.3 %copy.22 = bf16[4,4,3,2,6,512]{5,0,4,3,2,1:T(4,128)(2,1)} copy(bf16[4,4,3,2,6,512]{5,3,1,4,2,0:T(2,128)(2,1)S(1)} %bitcast.22) | data formatting | bytes 1179648 | tf_op jit(solution)/shard_map/transpose | solution.py:249
  (7 shorter events, 0.1 us)
Async XLA Ops:
  0.0 3.6 %copy-start.2 = (f32[2,512]{1,0:T(2,128)S(1)}, f32[2,512]{1,0:T(2,128)}, u32[]{:S(2)}) copy-start(f32[2,512]{1,0:T(2,128)} %g2_ref.1) | copy-start | bytes 12292
  0.0 3.6 %copy-start = (bf16[2,512,512]{2,1,0:T(8,128)(2,1)S(1)}, bf16[2,512,512]{2,1,0:T(8,128)(2,1)}, u32[]{:S(2)}) copy-start(bf16[2,512,512]{2,1,0:T(8,128)(2,1)} %wproj_hbm.1) | copy-start | bytes 3145732
  0.0 3.6 %copy-start.1 = (f32[2,512]{1,0:T(2,128)S(1)}, f32[2,512]{1,0:T(2,128)}, u32[]{:S(2)}) copy-start(f32[2,512]{1,0:T(2,128)} %g1_ref.1) | copy-start | bytes 12292

commit v3 on v2

--- a/solution.py
+++ b/solution.py
@@ -91,10 +91,17 @@
             device_id=before[towards], device_id_type=MESH,
         )
 
+    row_count, chunk = back.shape[2:4]
+
+    def home(atom):
+        return out_ref.at[
+            pl.ds(atom // 2 * row_count, row_count), pl.ds(atom % 2 * chunk, chunk), :
+        ]
+
     def backward_copy(at):
         atom, window, place, towards = moves[at]
         return pltpu.make_async_remote_copy(
-            back.at[window, place], out_ref.at[atom], bsend.at[at], brecv.at[at],
+            back.at[window, place], home(atom), bsend.at[at], brecv.at[at],
             device_id=after[towards], device_id_type=MESH,
         )
 
@@ -155,14 +162,21 @@
         for column in range(0, hidden, step):
             inner = gelu(dot(n2, wup[block, :, column : column + step])).astype(BF16)
             h = h + dot(inner, wdown[block, column : column + step, :])
-        return h[:atom_size].astype(BF16), h[atom_size:].astype(BF16)
+        return h[:atom_size], h[atom_size:]
 
     def prepare_first(u):
         atoms = (4 * u, 4 * u + 2, 4 * u + 1, 4 * u + 3)
-        prepare(0, u, [x_ref[a] for a in atoms], [e_ref[a] for a in atoms])
+        pieces = [
+            x_ref[a // 2 * row_count + row, a % 2 * chunk : (a % 2 + 1) * chunk, :]
+            for a in atoms
+            for row in range(row_count)
+        ]
+        prepare(0, u, pieces, [e_ref[a] for a in atoms])
 
     def part_first(u, which, first=False):
-        own[4 * u + which], own[4 * u + 2 + which] = part(0, u, which, first)
+        results = part(0, u, which, first)
+        own[4 * u + which] = results[0].astype(BF16)
+        own[4 * u + 2 + which] = results[1].astype(BF16)
 
     prepare_first(0)
     weights[2].start()
@@ -172,12 +186,12 @@
     for at in range(5):
         label_copy(at).start()
     forward_copy(0).start()
-    forward_copy(1).start()
     for at in range(4, 8):
         weights[at].start()
     prepare_first(1)
     part_first(1, 0)
     forward_copy(2).start()
+    forward_copy(1).start()
     forward_copy(3).start()
     part_first(0, 1)
     forward_copy(4).start()
@@ -202,10 +216,15 @@
         results = part(1, w, which, first)
         for at in range(2):
             place = 2 * which + at
-            if (w, place) in local:
-                out_ref[local[w, place]] = results[at]
-            else:
-                back[w, place] = results[at]
+            for row in range(row_count):
+                piece = results[at][row * chunk : (row + 1) * chunk].astype(BF16)
+                if (w, place) in local:
+                    atom = local[w, place]
+                    out_ref[
+                        atom // 2 * row_count + row, atom % 2 * chunk : (atom % 2 + 1) * chunk, :
+                    ] = piece
+                else:
+                    back[w, place, row] = piece
         for at in range(2):
             if (w, 2 * which + at) in arrivals:
                 backward_copy(arrivals[w, 2 * which + at]).start()
@@ -224,66 +243,41 @@
         backward_copy(at).wait_send()
 
 
-def to_atoms(field):
-    levels, row_count, column_count = field.shape[:3]
-    trailing = tuple(field.shape[3:])
-    half_row, half_column = WLAT // 2, WLON // 2
-    shaped = field.reshape(
-        (levels, row_count // half_row, half_row, column_count // half_column, half_column)
-        + trailing
-    )
-    order = (1, 3, 0, 2, 4) + tuple(range(5, 5 + len(trailing)))
-    return jnp.transpose(shaped, order).reshape(
-        (-1, levels * half_row * half_column) + trailing
-    )
-
-
-def from_atoms(atoms, levels, row_count, column_count):
-    trailing = tuple(atoms.shape[2:])
-    half_row, half_column = WLAT // 2, WLON // 2
-    shaped = atoms.reshape(
-        (row_count // half_row, column_count // half_column, levels, half_row, half_column)
-        + trailing
-    )
-    order = (2, 0, 3, 1, 4) + tuple(range(5, 5 + len(trailing)))
-    return jnp.transpose(shaped, order).reshape((levels, row_count, column_count) + trailing)
-
-
 def per_device(
     tokens, region, norm_gain1, qkv_weight, proj_weight, norm_gain2, up_weight, down_weight
 ):
     levels, row_count, column_count, features = tokens.shape
-    hidden = up_weight.shape[2]
-    x = to_atoms(tokens)
-    atoms, size, _ = x.shape
+    half_row, half_column = WLAT // 2, WLON // 2
+    groups, halves = row_count // half_row, column_count // half_column
+    atoms, chunk = groups * halves, half_column * levels
+    size = half_row * chunk
     span = 4 * size
-
-    level = jnp.arange(levels, dtype=jnp.int32)[:, None, None]
-    row = (lax.axis_index("lat") * row_count + jnp.arange(row_count, dtype=jnp.int32))[None, :, None]
-    pair_first = level // WLEV
+    x = jnp.transpose(tokens, (1, 2, 0, 3)).reshape(row_count, column_count * levels, features)
+
+    region = jnp.transpose(region, (1, 2, 0)).reshape(groups, half_row, halves, chunk)
+    region = jnp.transpose(region, (0, 2, 1, 3)).reshape(atoms, size, 1)
+    shape = (atoms, size, 128)
+    level = lax.broadcasted_iota(jnp.int32, shape, 1) % levels
     rolled_level = (level + levels - WLEV // 2) % levels
     wrapped_level = (rolled_level >= levels - WLEV // 2).astype(jnp.int32)
-    wrapped_row = (row < WLAT // 2).astype(jnp.int32)
-    first_class = region * 2 + pair_first
+    top = lax.broadcasted_iota(jnp.int32, shape, 0) < halves
+    wrapped_row = (top & (lax.axis_index("lat") == 0)).astype(jnp.int32)
+    first_class = region * 2 + level // WLEV
     second_class = ((region * 2 + rolled_level // WLEV) * 2 + wrapped_level) * 2 + wrapped_row
-    classes = jnp.stack([first_class, second_class + 64], axis=-1)
-    classes = to_atoms(classes)
-    lane = jnp.arange(128, dtype=jnp.int32)
-    marks = (
-        (classes[:, :, :1] == lane) | (classes[:, :, 1:] == lane)
-    ).astype(BF16)
+    lane = lax.broadcasted_iota(jnp.int32, shape, 2)
+    marks = ((lane == first_class) | (lane == second_class + 64)).astype(BF16)
 
     vmem = pl.BlockSpec(memory_space=pltpu.VMEM)
     hbm = pl.BlockSpec(memory_space=pl.ANY)
     out = pl.pallas_call(
         kernel,
-        out_shape=jax.ShapeDtypeStruct((atoms, size, features), BF16),
+        out_shape=jax.ShapeDtypeStruct(x.shape, BF16),
         in_specs=[vmem] * 4 + [hbm] * 4,
         out_specs=vmem,
         scratch_shapes=[
             pltpu.VMEM((atoms, size, features), BF16),
             pltpu.VMEM((2, 4, size, features), BF16),
-            pltpu.VMEM((2, 4, size, features), BF16),
+            pltpu.VMEM((2, 4, half_row, chunk, features), BF16),
             pltpu.VMEM((2, 4, size, 128), BF16),
             pltpu.VMEM((4, span, features), F32),
             pltpu.VMEM((4, span, 3 * features), BF16),
@@ -305,7 +299,8 @@
             collective_id=0, has_side_effects=True, vmem_limit_bytes=50 * 1024 * 1024
         ),
     )(x, marks, norm_gain1, norm_gain2, qkv_weight, proj_weight, up_weight, down_weight)
-    return from_atoms(out, levels, row_count, column_count)
+    out = out.reshape(row_count, column_count, levels, features)
+    return jnp.transpose(out, (2, 0, 1, 3))
 
 
 def solution(mesh):

time: 38.3 us -> 39.5 us (1.031)
  local copies, waits for them, and re-layouts: 4.03 us -> 5.34 us
    unnamed x6, local copies, waits for them, and re-layouts: 0.01 us -> 2.59 us
    transpose x1 -> x0, local copies, waits for them, and re-layouts: 1.27 us -> none  [from_atoms(): jnp.transpose(shaped, order)]
    add x1 -> x0, other arithmetic: 0.91 us -> none  [per_device(): first_class = region * 2 + pair_first]
    mul x0 -> x1, other arithmetic: none -> 0.75 us  [per_device(): first_class = region * 2 + level // WLEV]
    reshape x5 -> x2, local copies, waits for them, and re-layouts: 2.33 us -> 2.41 us  [the longest x1 1.45 us: per_device(): jnp.transpose(tokens, (1, 2, 0, 3))]
where the time goes in v3:
time: 39.5 us; the launch traced here: 39.1 us
  Pallas kernels  32.7 us (83%)
  local copies, waits for them, and re-layouts  5.34 us (14%)
  other arithmetic  1.01 us (3%)
    pallas_call x1, Pallas kernels, per_device(): pl.pallas_call(kernel, out_shape=jax.ShapeDtypeStruct(x.shape, BF16), in_...  32.7 us
    unnamed x6, local copies, waits for them, and re-layouts  2.59 us
    reshape x1, local copies, waits for them, and re-layouts, per_device(): jnp.transpose(tokens, (1, 2, 0, 3))  1.45 us
    reshape x1, local copies, waits for them, and re-layouts, per_device(): out = out.reshape(row_count, column_count, levels, features)  0.95 us

profile of v3, /device:TPU:0, one launch (start us, length us, event | category | flops | bytes accessed | tf_op | source)
XLA Modules:
  0.0 39.1 jit_solution(11065996198193072656)
XLA Ops:
  0.0 0.7 %multiply_bitcast_fusion = s32[12,12,4]{1,2,0:T(4,128)S(1)} fusion(s32[4,12,12]{2,0,1:T(4,128)} %param.9), kind=kLoop, calls=%fused_computation.37 | loop fusion | flops 576 | bytes 4608 | tf_op jit(solution)/shard_map/mul | solution.py:265
  0.8 0.2 copy.9
  0.9 0.1 mul.29
  1.0 0.1 mul.31
  1.1 0.2 fusion.20.e_ref
  1.4 1.5 %reshape.19.x_ref = bf16[12,48,512]{2,1,0:T(8,128)(2,1)S(1)} reshape(bf16[12,12,4,512]{3,2,1,0:T(4,128)(2,1)} %bitcast.5) | data formatting | bytes 1179648 | tf_op jit(solution)/shard_map/reshape | solution.py:255
  2.8 0.0 copy-start
  2.8 1.2 %copy-done = bf16[2,512,512]{2,1,0:T(8,128)(2,1)S(1)} copy-done((bf16[2,512,512]{2,1,0:T(8,128)(2,1)S(1)}, bf16[2,512,512]{2,1,0:T(8,128)(2,1)}, u32[]{:S(2)}) %copy-start) | copy-done | bytes 1048600
  4.1 0.0 copy-start.1
  4.1 0.7 %copy-done.1 = f32[2,512]{1,0:T(2,128)S(1)} copy-done((f32[2,512]{1,0:T(2,128)S(1)}, f32[2,512]{1,0:T(2,128)}, u32[]{:S(2)}) %copy-start.1) | copy-done | bytes 4120
  4.8 0.0 copy-start.2
  4.8 0.7 %copy-done.2 = f32[2,512]{1,0:T(2,128)S(1)} copy-done((f32[2,512]{1,0:T(2,128)S(1)}, f32[2,512]{1,0:T(2,128)}, u32[]{:S(2)}) %copy-start.2) | copy-done | bytes 4120
  5.4 32.7 %shard_map.82 = bf16[12,48,512]{2,1,0:T(8,128)(2,1)S(1)} custom-call(bf16[12,48,512]{2,1,0:T(8,128)(2,1)S(1)} %reshape.19.x_ref, bf16[8,72,128]{2,1,0:T(8,128)(2,1)S(1)} %fusion.20.e_ref, f32[2,512]{1,0:T(2,128)S(1)} %copy-done.1, f32[2,512]{1,0:T(2,128)S(1)} %copy-done.2, bf16[2,512,1536]{2,1,0:T(8,128)(2,1)} %wqkv_hbm.1, bf16[2,512,512]{2,1,0:T(8,128)(2,1)S(1)} %copy-done, ...), custom_call_target="tpu_custom_call" | custom-call | tf_op jit(solution)/shard_map/pallas_call | solution.py:272
  38.2 1.0 %reshape.20 = bf16[12,12,4,512]{3,2,1,0:T(4,128)(2,1)} reshape(bf16[12,48,512]{2,1,0:T(8,128)(2,1)S(1)} %shard_map.82) | data formatting | bytes 1179648 | tf_op jit(solution)/shard_map/reshape | solution.py:302
  (4 shorter events, 0.0 us)
Async XLA Ops:
  2.8 1.2 %copy-start = (bf16[2,512,512]{2,1,0:T(8,128)(2,1)S(1)}, bf16[2,512,512]{2,1,0:T(8,128)(2,1)}, u32[]{:S(2)}) copy-start(bf16[2,512,512]{2,1,0:T(8,128)(2,1)} %wproj_hbm.1) | copy-start | bytes 3145732
  4.1 0.7 %copy-start.1 = (f32[2,512]{1,0:T(2,128)S(1)}, f32[2,512]{1,0:T(2,128)}, u32[]{:S(2)}) copy-start(f32[2,512]{1,0:T(2,128)} %g1_ref.1) | copy-start | bytes 12292
  4.8 0.7 %copy-start.2 = (f32[2,512]{1,0:T(2,128)S(1)}, f32[2,512]{1,0:T(2,128)}, u32[]{:S(2)}) copy-start(f32[2,512]{1,0:T(2,128)} %g2_ref.1) | copy-start | bytes 12292
